TPU v7x, 128 devices: a whole 4x4x4 slice. The times are simulated.
128 devices in a mesh: dp: 16 (over y, x_lo, core), shard: 8 (over z, x_hi).
Axes of the slice: x: 4 (x_hi: 2, x_lo: 2; x = x_hi * 2 + x_lo), y: 4, z: 4, core: 2. Of those that a mesh axis runs over, the one named last changes fastest.
Arguments:
- gradients: bfloat16 [16, 88, 512, 512], P('dp', 'shard'), may hold values from -60 to 60
- owners: int32 [8, 11], P('shard'), may hold values from 0 to 15, as said below
- block_param: int32 [88], replicated, may hold values from 0 to 6, never falling along the last dimension, each value on 1 to 25 neighbouring positions
- left_stat: float32 [32, 8, 512, 512], P('dp', 'shard'), may hold values from -4 to 8, as said below
- right_stat: float32 [32, 8, 512, 512], P('dp', 'shard'), may hold values from -4 to 8, as said below
- moment: float32 [32, 8, 512, 512], P('dp', 'shard'), may hold values from 0.5 to 50
- left_root: bfloat16 [32, 8, 512, 512], P('dp', 'shard'), may hold values from -1 to 3.5, as said below
- right_root: bfloat16 [32, 8, 512, 512], P('dp', 'shard'), may hold values from -1 to 3.5, as said below
Outputs:
- new_left: float32 [32, 8, 512, 512], P('dp', 'shard')
- new_right: float32 [32, 8, 512, 512], P('dp', 'shard')
- new_moment: float32 [32, 8, 512, 512], P('dp', 'shard')
- update: bfloat16 [88, 512, 512], P('shard')
Inputs may be any that keep to these rules, and one draw needn't show every extreme that they name: `owners`: in each row, no value occurs more than 2 times, and some value occurs exactly 2 times. `left_stat`: each slot's matrix is symmetric. `right_stat`: each slot's matrix is symmetric. `left_root`: each slot's matrix is symmetric. `right_root`: each slot's matrix is symmetric.
All inputs are finite; a program needn't handle non-finite values.
Results may differ from a plain program's by a relative error of at most 0.0058.
Values may be sent and summed in bfloat16 or wider, within the bound.
A program may use at most 192 MiB of HBM per device.

v0:
```python
import jax
import jax.numpy as jnp
from jax import lax
from jax.sharding import Mesh
from jax.sharding import PartitionSpec as P

NPARAM = 7
DP = ("dp_0", "dp_1", "dp_2")
SHARD = ("shard_0", "shard_1")
DP_SHARD = ("dp_0", "dp_1", "dp_2", "shard_0", "shard_1")
decay_rate = 0.95
tiny_value = 1e-06


def by_axis(x, axes):
    for axis in axes:
        x = lax.psum(x, axis)
    return x


def on_device(gradients, owners, block_param, left_stat, right_stat, moment, left_root, right_root):
    replicas = lax.axis_size(DP)
    capacity = left_stat.shape[0]
    blocks = gradients.shape[1]
    block_width = gradients.shape[3]
    device = lax.axis_index(DP)
    column = lax.axis_index(SHARD)
    owner_row = owners[0]
    counter = jnp.arange(blocks, dtype=jnp.int32)
    same_owner = owner_row[:, None] == owner_row[None, :]
    earlier = counter[None, :] < counter[:, None]
    places = owner_row * capacity + jnp.sum(jnp.where(same_owner & earlier, 1, 0), axis=1).astype(
        jnp.int32
    )
    slot_ids = jnp.arange(replicas * capacity, dtype=jnp.int32)
    matches = places[None, :] == slot_ids[:, None]
    source = jnp.min(jnp.where(matches, counter[None, :], blocks), axis=1)
    partials = gradients[0].astype(jnp.float32)
    row_share = lax.psum_scatter(partials, DP, scatter_dimension=1, tiled=True)
    share_padded = jnp.concatenate(
        [row_share, jnp.zeros((1,) + row_share.shape[1:], jnp.float32)], axis=0
    )
    outgoing = jnp.take(share_padded, source, axis=0).reshape(
        replicas, capacity, block_width // replicas, block_width
    )
    arrived = lax.all_to_all(outgoing, DP, split_axis=0, concat_axis=2, tiled=True)
    summed = arrived[0]
    left_gram = jnp.einsum("cij,ckj->cik", summed, summed, precision=lax.Precision.HIGHEST)
    right_gram = jnp.einsum("cji,cjk->cik", summed, summed, precision=lax.Precision.HIGHEST)
    new_left = decay_rate * left_stat + (1.0 - decay_rate) * left_gram[:, None]
    new_right = decay_rate * right_stat + (1.0 - decay_rate) * right_gram[:, None]
    new_moment = decay_rate * moment + (1.0 - decay_rate) * (summed * summed)[:, None]
    adam_step = summed / (jnp.sqrt(new_moment[:, 0]) + tiny_value)
    left_half = jnp.einsum(
        "cij,cjk->cik",
        left_root[:, 0],
        summed.astype(jnp.bfloat16),
        preferred_element_type=jnp.float32,
    ).astype(jnp.bfloat16)
    direction = jnp.einsum(
        "cij,cjk->cik", left_half, right_root[:, 0], preferred_element_type=jnp.float32
    )
    my_slots = lax.dynamic_slice_in_dim(matches, device * capacity, capacity, 0)
    local_params = lax.dynamic_slice_in_dim(block_param, column * blocks, blocks, 0)
    slot_param = jnp.sum(jnp.where(my_slots, local_params[None, :], 0), axis=1)
    is_live = jnp.any(my_slots, axis=1)
    param_ids = jnp.arange(NPARAM, dtype=jnp.int32)
    member = (slot_param[:, None] == param_ids[None, :]) & is_live[:, None]
    adam_squares = jnp.sum(adam_step * adam_step, axis=(1, 2))
    direction_squares = jnp.sum(direction * direction, axis=(1, 2))
    adam_local = jnp.sum(jnp.where(member, adam_squares[:, None], 0.0), axis=0)
    direction_local = jnp.sum(jnp.where(member, direction_squares[:, None], 0.0), axis=0)
    adam_norm, direction_norm = (by_axis(adam_local, DP_SHARD), by_axis(direction_local, DP_SHARD))
    graft_ratio = jnp.sqrt((adam_norm + tiny_value) / (direction_norm + tiny_value))
    slot_ratio = jnp.sum(jnp.where(member, graft_ratio[None, :], 0.0), axis=1)
    slot_update = (slot_ratio[:, None, None] * direction).astype(jnp.bfloat16)
    returned = lax.all_to_all(slot_update, DP, split_axis=1, concat_axis=0, tiled=True)
    pieces = jnp.take(returned, places, axis=0)
    update = lax.all_gather(pieces, DP, axis=1, tiled=True)
    return (new_left, new_right, new_moment, update)


def solution(mesh):
    finer = Mesh(
        mesh.devices.reshape(4, 2, 2, 4, 2), ("dp_0", "dp_1", "dp_2", "shard_0", "shard_1")
    )
    placed = (
        P(DP, SHARD, None, None),
        P(SHARD, None),
        P(),
        P(DP, SHARD, None, None),
        P(DP, SHARD, None, None),
        P(DP, SHARD, None, None),
        P(DP, SHARD, None, None),
        P(DP, SHARD, None, None),
    )
    return jax.shard_map(
        on_device,
        mesh=finer,
        in_specs=placed,
        out_specs=(
            P(DP, SHARD, None, None),
            P(DP, SHARD, None, None),
            P(DP, SHARD, None, None),
            P(SHARD, None, None),
        ),
        check_vma=False,
    )
```

profile of v0, /device:TPU:1, one launch (start us, length us, event | category | flops | bytes accessed | tf_op | source)
XLA Modules:
  0.0 309.6 jit_solution(17516869295652060086)
XLA Ops:
  7.2 0.0 copy-start
  7.2 0.0 reduce-scatter.2.cloned.1.call-start
  7.2 8.7 %bitcast_convert_fusion = f32[11,512,512]{2,1,0:T(8,128)} fusion(bf16[1,11,512,512]{3,2,1,0:T(8,128)(2,1)} %param.8), kind=kLoop, calls=%fused_computation.2 | loop fusion | flops 2883584 | bytes 17301504 | tf_op jit(solution)/shard_map/convert_element_type | solution.py:38
  15.9 0.0 reduce-scatter.2.cloned.1.call-update
  15.9 0.6 copy-done.6
  16.6 0.2 select_reduce_fusion.1
  16.7 0.1 select_reduce_fusion
  16.9 0.1 reduce_min.14
  17.0 130.2 %reduce-scatter.2.cloned.1.call-done = f32[11,32,512]{2,1,0:T(8,128)} async-done(((f32[11,512,512]{2,1,0:T(8,128)}), f32[11,32,512]{2,1,0:T(8,128)}) %reduce-scatter.2.cloned.1.call-update) | async-done | bytes 720912 | tf_op jit(solution)/shard_map/reduce_scatter | solution.py:39
  147.2 1.2 concatenate.3
  148.4 2.0 gather_fusion
  150.4 3.1 %broadcast_select_fusion = f32[16,2,32,512]{3,2,1,0:T(8,128)} fusion(f32[16,2,32,512]{3,2,1,0:T(8,128)} %bitcast.83, pred[16,2]{1,0:T(8,128)(4,1)S(1)} %compare_and_fusion), kind=kLoop, calls=%fused_computation.23 | loop fusion | flops 524288 | bytes 4194336 | tf_op jit(solution)/shard_map/jit(_take)/select_n | solution.py:43
  153.5 5.9 %all-to-all-start = ((f32[16,2,32,512]{3,2,1,0:T(8,128)}), f32[16,2,32,512]{3,2,1,0:T(8,128)S(1)}, u32[]{:S(2)}, u32[]{:S(2)}) async-start(f32[16,2,32,512]{3,2,1,0:T(8,128)} %broadcast_select_fusion), calls=%async_computation.1 | async-start | bytes 4194304 | tf_op jit(solution)/shard_map/all_to_all | solution.py:46
  159.3 0.1 dynamic_slice.7
  159.4 0.1 fusion.15
  159.5 0.1 select_reduce_fusion.5
  159.7 26.7 %all-to-all-done = f32[16,2,32,512]{3,2,1,0:T(8,128)S(1)} async-done(((f32[16,2,32,512]{3,2,1,0:T(8,128)}), f32[16,2,32,512]{3,2,1,0:T(8,128)S(1)}, u32[]{:S(2)}, u32[]{:S(2)}) %all-to-all-start) | async-done | bytes 2097184 | tf_op jit(solution)/shard_map/all_to_all | solution.py:46
  186.4 0.3 multiply_multiply_fusion
  186.6 1.1 copy-done.2
  187.7 0.2 copy.65
  187.9 0.0 copy-start.3
  188.0 2.0 copy.61
  189.9 0.3 copy-done.3
  190.2 2.8 sqrt_add_fusion
  193.0 4.0 %multiply_reduce_fusion = (f32[2]{0:T(128)S(1)}, f32[2,512,512]{2,1,0:T(8,128)}) fusion(bf16[2,1,512,512]{3,2,1,0:T(8,128)(2,1)S(1)} %copy-done, bf16[2,1,512,512]{3,2,1,0:T(8,128)(2,1)} %param.14, f32[2,512,512]{2,1,0:T(8,128)S(1)} %bitcast.79), kind=kOutput, calls=%fused_computation.14 | convolution fusion | flops 1075838976 | bytes 6291464 | tf_op jit(solution)/shard_map/cij,cjk->cik/dot_general | solution.py:60
  197.0 2.7 fusion.3
  199.6 0.1 select_reduce_fusion.4
  199.7 7.2 %all-reduce.2 = (f32[7]{0:T(128)S(1)}, f32[7]{0:T(128)S(1)}) all-reduce(f32[7]{0:T(128)S(1)} %get-tuple-element.25, f32[7]{0:T(128)S(1)} %get-tuple-element.24), channel_id=1, replica_groups=mesh['dp_0'=4,'dp_1'=2,'dp_2'=2,'shard_0'=4,'shard_1'=2] {'dp_0'}, use_global_device_ids=true, to_apply=%region_14.15 | all-reduce | flops 14 | bytes 112 | tf_op jit(solution)/shard_map/psum | solution.py:17
  206.9 3.8 %all-reduce.5 = (f32[7]{0:T(128)S(1)}, f32[7]{0:T(128)S(1)}) all-reduce(f32[7]{0:T(128)S(1)} %get-tuple-element.28, f32[7]{0:T(128)S(1)} %get-tuple-element.29), channel_id=1, replica_groups=mesh['dp_0'=4,'dp_1'=2,'dp_2'=2,'shard_0'=4,'shard_1'=2] {'dp_1'}, use_global_device_ids=true, to_apply=%region_15.16 | all-reduce | flops 14 | bytes 112 | tf_op jit(solution)/shard_map/psum | solution.py:17
  210.7 6.2 %all-reduce.4 = (f32[7]{0:T(128)S(1)}, f32[7]{0:T(128)S(1)}) all-reduce(f32[7]{0:T(128)S(1)} %get-tuple-element.34, f32[7]{0:T(128)S(1)} %get-tuple-element.35), channel_id=1, replica_groups=mesh['dp_0'=4,'dp_1'=2,'dp_2'=2,'shard_0'=4,'shard_1'=2] {'dp_2'}, use_global_device_ids=true, to_apply=%region_16.17 | all-reduce | flops 14 | bytes 112 | tf_op jit(solution)/shard_map/psum | solution.py:17
  216.9 8.7 %all-reduce.1 = (f32[7]{0:T(128)S(1)}, f32[7]{0:T(128)S(1)}) all-reduce(f32[7]{0:T(128)S(1)} %get-tuple-element.32, f32[7]{0:T(128)S(1)} %get-tuple-element.33), channel_id=1, replica_groups=mesh['dp_0'=4,'dp_1'=2,'dp_2'=2,'shard_0'=4,'shard_1'=2] {'shard_0'}, use_global_device_ids=true, to_apply=%region_17.18 | all-reduce | flops 14 | bytes 112 | tf_op jit(solution)/shard_map/psum | solution.py:17
  225.6 5.3 %all-reduce.3 = (f32[7]{0:T(128)S(1)}, f32[7]{0:T(128)S(1)}) all-reduce(f32[7]{0:T(128)S(1)} %get-tuple-element.26, f32[7]{0:T(128)S(1)} %get-tuple-element.27), channel_id=1, replica_groups=mesh['dp_0'=4,'dp_1'=2,'dp_2'=2,'shard_0'=4,'shard_1'=2] {'shard_1'}, use_global_device_ids=true, to_apply=%region_18.19 | all-reduce | flops 14 | bytes 112 | tf_op jit(solution)/shard_map/psum | solution.py:17
  230.9 0.2 select_reduce_fusion.2
  231.1 1.9 multiply_convert_fusion
  233.0 2.0 copy.69
  235.0 7.0 %all-to-all-start.1 = ((bf16[2,512,512]{2,0,1:T(2,128)(2,1)}), bf16[2,512,512]{2,0,1:T(2,128)(2,1)S(1)}, u32[]{:S(2)}, u32[]{:S(2)}) async-start(bf16[2,512,512]{2,0,1:T(2,128)(2,1)} %copy.69), calls=%async_computation.2 | async-start | bytes 2097152 | tf_op jit(solution)/shard_map/all_to_all | solution.py:77
  242.0 0.2 all-gather.2.cloned.1.call-start
  242.2 15.5 %all-to-all-done.1 = bf16[2,512,512]{2,0,1:T(2,128)(2,1)S(1)} async-done(((bf16[2,512,512]{2,0,1:T(2,128)(2,1)}), bf16[2,512,512]{2,0,1:T(2,128)(2,1)S(1)}, u32[]{:S(2)}, u32[]{:S(2)}) %all-to-all-start.1) | async-done | bytes 1048608 | tf_op jit(solution)/shard_map/all_to_all | solution.py:77
  257.7 0.2 copy.70
  257.9 0.1 copy.71
  258.0 0.6 gather_fusion.1
  258.6 0.8 broadcast_select_fusion.1
  259.4 0.0 all-gather.2.cloned.1.call-update
  259.4 0.0 copy-start.4
  259.4 6.1 %fusion = f32[2,1,512,512]{3,2,1,0:T(8,128)} fusion(f32[2,1,512,512]{3,2,1,0:T(8,128)} %param.12, f32[2,512,512]{2,1,0:T(8,128)S(1)} %bitcast.80), kind=kOutput, calls=%fused_computation.6 | convolution fusion | flops 3222798336 | bytes 6291456 | tf_op jit(solution)/shard_map/cji,cjk->cik/dot_general | solution.py:49
  265.6 5.0 %fusion.1 = f32[2,1,512,512]{3,2,1,0:T(8,128)} fusion(f32[2,1,512,512]{3,2,1,0:T(8,128)S(1)} %copy-done.4, f32[2,512,512]{2,1,0:T(8,128)S(1)} %bitcast.81), kind=kOutput, calls=%fused_computation.9 | convolution fusion | flops 3222798336 | bytes 6291456 | tf_op jit(solution)/shard_map/cij,ckj->cik/dot_general | solution.py:48
  270.6 26.5 %all-gather.2.cloned.1.call-done = bf16[11,512,512]{2,1,0:T(8,128)(2,1)} async-done(((bf16[11,32,512]{2,1,0:T(8,128)(2,1)}), bf16[11,512,512]{2,1,0:T(8,128)(2,1)}) %all-gather.2.cloned.1.call-update) | async-done | bytes 5767184 | tf_op jit(solution)/shard_map/all_gather | solution.py:79
  297.1 5.6 %copy.85 = bf16[11,512,512]{2,1,0:T(8,128)(2,1)} copy(bf16[11,512,512]{2,1,0:T(8,128)(2,1)} %all-gather.2.cloned.1.call-done) | data formatting | bytes 11534336
  (17 shorter events, 0.1 us)
Async XLA Ops:
  7.2 185.8 %copy-start = (bf16[2,1,512,512]{3,2,1,0:T(8,128)(2,1)S(1)}, bf16[2,1,512,512]{3,2,1,0:T(8,128)(2,1)}, u32[]{:S(2)}) copy-start(bf16[2,1,512,512]{3,2,1,0:T(8,128)(2,1)} %param.15) | copy-start | bytes 3145732
  7.2 140.0 %reduce-scatter.2.cloned.1.call-start = ((), (), s32[]{:S(2)}) async-start(), calls=%async_computation.3 | async-start | bytes 12255232 | tf_op jit(solution)/shard_map/reduce_scatter | solution.py:39
  15.9 0.7 copy-start.6
  153.5 5.9 %copy-start.5 = (s32[88]{0:T(128)S(1)}, s32[88]{0:T(128)}, u32[]{:S(2)}) copy-start(s32[88]{0:T(128)} %param.10) | copy-start | bytes 1060
  153.5 32.9 %all-to-all-start = ((f32[16,2,32,512]{3,2,1,0:T(8,128)}), f32[16,2,32,512]{3,2,1,0:T(8,128)S(1)}, u32[]{:S(2)}, u32[]{:S(2)}) async-start(f32[16,2,32,512]{3,2,1,0:T(8,128)} %broadcast_select_fusion), calls=%async_computation.1 | async-start | bytes 4194304 | tf_op jit(solution)/shard_map/all_to_all | solution.py:46
  186.4 1.3 copy-start.2
  187.9 2.2 copy-start.3
  235.0 22.7 %all-to-all-start.1 = ((bf16[2,512,512]{2,0,1:T(2,128)(2,1)}), bf16[2,512,512]{2,0,1:T(2,128)(2,1)S(1)}, u32[]{:S(2)}, u32[]{:S(2)}) async-start(bf16[2,512,512]{2,0,1:T(2,128)(2,1)} %copy.69), calls=%async_computation.2 | async-start | bytes 2097152 | tf_op jit(solution)/shard_map/all_to_all | solution.py:77
  242.0 55.1 %all-gather.2.cloned.1.call-start = ((), (), s32[]{:S(2)}) async-start(), calls=%async_computation.4 | async-start | bytes 6127616 | tf_op jit(solution)/shard_map/all_gather | solution.py:79
  259.4 6.2 %copy-start.4 = (f32[2,1,512,512]{3,2,1,0:T(8,128)S(1)}, f32[2,1,512,512]{3,2,1,0:T(8,128)}, u32[]{:S(2)}) copy-start(f32[2,1,512,512]{3,2,1,0:T(8,128)} %param.11) | copy-start | bytes 6291460
  297.1 5.6 %copy-start.1 = (bf16[2,1,512,512]{3,2,1,0:T(8,128)(2,1)S(1)}, bf16[2,1,512,512]{3,2,1,0:T(8,128)(2,1)}, u32[]{:S(2)}) copy-start(bf16[2,1,512,512]{3,2,1,0:T(8,128)(2,1)} %param.15) | copy-start | bytes 3145732
Sparse Core Ops, SparseCore 0:
  16.0 131.0 reduce-scatter.1
  259.6 37.5 all-gather.1
where the time goes:
time: 310 us
  waiting for transfers between devices  199 us (64%)
  blocking collectives  31.1 us (10%)
  other arithmetic  21.1 us (7%)
  local copies, waits for them, and re-layouts  16 us (5%)
  matrix products  15.1 us (5%)
  between operations  14.2 us (5%)
  starting transfers between devices  13.1 us (4%)
    reduce_scatter x1, waiting for transfers between devices, on_device(): row_share = lax.psum_scatter(partials, DP, scatter_dimension=1, tiled=True)  130 us
    psum x5, blocking collectives, by_axis(): x = lax.psum(x, axis)  31.1 us
    all_to_all x1, waiting for transfers between devices, on_device(): lax.all_to_all(outgoing, DP, split_axis=0, concat_axis=2, tiled=True)  26.7 us
    all_gather x1, waiting for transfers between devices, on_device(): update = lax.all_gather(pieces, DP, axis=1, tiled=True)  26.5 us
    all_to_all x1, waiting for transfers between devices, on_device(): lax.all_to_all(slot_update, DP, split_axis=1, concat_axis=0, tiled=True)  15.5 us
    convert_element_type x1, other arithmetic, on_device(): partials = gradients[0].astype(jnp.float32)  8.67 us
    unnamed x15, local copies, waits for them, and re-layouts  7.59 us
    all_to_all x1, starting transfers between devices, on_device(): lax.all_to_all(slot_update, DP, split_axis=1, concat_axis=0, tiled=True)  6.96 us
  transfers between devices with their start and end apart: 4, of which 4 were waited for; matrix products, arithmetic and copies ran while one was open for 4% of the time, Pallas kernels for 0%

commit v1 on v0

--- a/solution.py
+++ b/solution.py
@@ -76,7 +76,9 @@
     slot_update = (slot_ratio[:, None, None] * direction).astype(jnp.bfloat16)
     returned = lax.all_to_all(slot_update, DP, split_axis=1, concat_axis=0, tiled=True)
     pieces = jnp.take(returned, places, axis=0)
-    update = lax.all_gather(pieces, DP, axis=1, tiled=True)
+    update = jnp.concatenate(
+        lax.all_to_all(jnp.stack([pieces] * lax.axis_size(DP)), DP, 0, 0), axis=1
+    )
     return (new_left, new_right, new_moment, update)
 
 

time: 310 us -> 347 us (1.12)
  waiting for transfers between devices: 199 us -> 228 us
  starting transfers between devices: 13.1 us -> 18.2 us
  local copies, waits for them, and re-layouts: 16 us -> 19.9 us
    all_to_all x0 -> x1, waiting for transfers between devices: none -> 55.3 us  [on_device(): lax.all_to_all(jnp.stack([pieces] * lax.axis_size(DP)), DP, 0, 0)]
    all_gather x1 -> x0, waiting for transfers between devices: 26.5 us -> none  [on_device(): update = lax.all_gather(pieces, DP, axis=1, tiled=True)]
    all_to_all x0 -> x1, local copies, waits for them, and re-layouts: none -> 6.25 us  [on_device(): lax.all_to_all(jnp.stack([pieces] * lax.axis_size(DP)), DP, 0, 0)]
    unnamed x15 -> x14, local copies, waits for them, and re-layouts: 7.59 us -> 1.96 us
    all_to_all x0 -> x1, starting transfers between devices: none -> 5.3 us  [on_device(): lax.all_to_all(jnp.stack([pieces] * lax.axis_size(DP)), DP, 0, 0)]
  transfers between devices with their start and end apart: 4 -> 4, of which waited for: 4 -> 4; matrix products, arithmetic and copies ran while one was open for 4% -> 3% of each run, Pallas kernels for 0% -> 0%
where the time goes in v1:
time: 347 us
  waiting for transfers between devices  228 us (66%)
  blocking collectives  31.1 us (9%)
  other arithmetic  20.4 us (6%)
  local copies, waits for them, and re-layouts  19.9 us (6%)
  starting transfers between devices  18.2 us (5%)
  matrix products  15.1 us (4%)
  between operations  14.2 us (4%)
    reduce_scatter x1, waiting for transfers between devices, on_device(): row_share = lax.psum_scatter(partials, DP, scatter_dimension=1, tiled=True)  130 us
    all_to_all x1, waiting for transfers between devices, on_device(): lax.all_to_all(jnp.stack([pieces] * lax.axis_size(DP)), DP, 0, 0)  55.3 us
    psum x5, blocking collectives, by_axis(): x = lax.psum(x, axis)  31.1 us
    all_to_all x1, waiting for transfers between devices, on_device(): lax.all_to_all(outgoing, DP, split_axis=0, concat_axis=2, tiled=True)  26.7 us
    all_to_all x1, waiting for transfers between devices, on_device(): lax.all_to_all(slot_update, DP, split_axis=1, concat_axis=0, tiled=True)  15.7 us
    convert_element_type x1, other arithmetic, on_device(): partials = gradients[0].astype(jnp.float32)  8.67 us
    all_to_all x1, starting transfers between devices, on_device(): lax.all_to_all(slot_update, DP, split_axis=1, concat_axis=0, tiled=True)  6.96 us
  transfers between devices with their start and end apart: 4, of which 4 were waited for; matrix products, arithmetic and copies ran while one was open for 3% of the time, Pallas kernels for 0%

profile of v1, /device:TPU:1, one launch (start us, length us, event | category | flops | bytes accessed | tf_op | source)
XLA Modules:
  0.0 346.8 jit_solution(11973509764930689594)
XLA Ops:
  7.2 0.0 copy-start
  7.2 0.0 reduce-scatter.2.cloned.1.call-start
  7.2 8.7 %bitcast_convert_fusion = f32[11,512,512]{2,1,0:T(8,128)} fusion(bf16[1,11,512,512]{3,2,1,0:T(8,128)(2,1)} %param.8), kind=kLoop, calls=%fused_computation.2 | loop fusion | flops 2883584 | bytes 17301504 | tf_op jit(solution)/shard_map/convert_element_type | solution.py:38
  15.9 0.0 reduce-scatter.2.cloned.1.call-update
  15.9 0.6 copy-done.6
  16.6 0.2 select_reduce_fusion.1
  16.7 0.1 select_reduce_fusion
  16.9 0.1 reduce_min.14
  17.0 130.2 %reduce-scatter.2.cloned.1.call-done = f32[11,32,512]{2,1,0:T(8,128)} async-done(((f32[11,512,512]{2,1,0:T(8,128)}), f32[11,32,512]{2,1,0:T(8,128)}) %reduce-scatter.2.cloned.1.call-update) | async-done | bytes 720912 | tf_op jit(solution)/shard_map/reduce_scatter | solution.py:39
  147.2 1.2 concatenate.3
  148.4 2.0 gather_fusion
  150.4 3.1 broadcast_select_fusion
  153.5 5.9 %all-to-all-start = ((f32[16,2,32,512]{3,2,1,0:T(8,128)}), f32[16,2,32,512]{3,2,1,0:T(8,128)S(1)}, u32[]{:S(2)}, u32[]{:S(2)}) async-start(f32[16,2,32,512]{3,2,1,0:T(8,128)} %broadcast_select_fusion), calls=%async_computation.1 | async-start | bytes 4194304 | tf_op jit(solution)/shard_map/all_to_all | solution.py:46
  159.3 0.1 dynamic_slice.7
  159.4 0.1 fusion.15
  159.5 0.1 select_reduce_fusion.5
  159.7 26.7 %all-to-all-done = f32[16,2,32,512]{3,2,1,0:T(8,128)S(1)} async-done(((f32[16,2,32,512]{3,2,1,0:T(8,128)}), f32[16,2,32,512]{3,2,1,0:T(8,128)S(1)}, u32[]{:S(2)}, u32[]{:S(2)}) %all-to-all-start) | async-done | bytes 2097184 | tf_op jit(solution)/shard_map/all_to_all | solution.py:46
  186.4 0.3 multiply_multiply_fusion
  186.6 1.1 copy-done.2
  187.7 0.2 copy.66
  187.9 0.0 copy-start.3
  188.0 2.0 copy.62
  189.9 0.3 copy-done.3
  190.2 2.8 sqrt_add_fusion
  193.0 4.0 %multiply_reduce_fusion = (f32[2]{0:T(128)S(1)}, f32[2,512,512]{2,1,0:T(8,128)}) fusion(bf16[2,1,512,512]{3,2,1,0:T(8,128)(2,1)S(1)} %copy-done, bf16[2,1,512,512]{3,2,1,0:T(8,128)(2,1)} %param.14, f32[2,512,512]{2,1,0:T(8,128)S(1)} %bitcast.82), kind=kOutput, calls=%fused_computation.14 | convolution fusion | flops 1075838976 | bytes 6291464 | tf_op jit(solution)/shard_map/cij,cjk->cik/dot_general | solution.py:60
  197.0 2.7 fusion.3
  199.6 0.1 select_reduce_fusion.4
  199.7 7.2 %all-reduce.2 = (f32[7]{0:T(128)S(1)}, f32[7]{0:T(128)S(1)}) all-reduce(f32[7]{0:T(128)S(1)} %get-tuple-element.25, f32[7]{0:T(128)S(1)} %get-tuple-element.24), channel_id=1, replica_groups=mesh['dp_0'=4,'dp_1'=2,'dp_2'=2,'shard_0'=4,'shard_1'=2] {'dp_0'}, use_global_device_ids=true, to_apply=%region_14.15 | all-reduce | flops 14 | bytes 112 | tf_op jit(solution)/shard_map/psum | solution.py:17
  206.9 3.8 %all-reduce.5 = (f32[7]{0:T(128)S(1)}, f32[7]{0:T(128)S(1)}) all-reduce(f32[7]{0:T(128)S(1)} %get-tuple-element.28, f32[7]{0:T(128)S(1)} %get-tuple-element.29), channel_id=1, replica_groups=mesh['dp_0'=4,'dp_1'=2,'dp_2'=2,'shard_0'=4,'shard_1'=2] {'dp_1'}, use_global_device_ids=true, to_apply=%region_15.16 | all-reduce | flops 14 | bytes 112 | tf_op jit(solution)/shard_map/psum | solution.py:17
  210.7 6.2 %all-reduce.4 = (f32[7]{0:T(128)S(1)}, f32[7]{0:T(128)S(1)}) all-reduce(f32[7]{0:T(128)S(1)} %get-tuple-element.34, f32[7]{0:T(128)S(1)} %get-tuple-element.35), channel_id=1, replica_groups=mesh['dp_0'=4,'dp_1'=2,'dp_2'=2,'shard_0'=4,'shard_1'=2] {'dp_2'}, use_global_device_ids=true, to_apply=%region_16.17 | all-reduce | flops 14 | bytes 112 | tf_op jit(solution)/shard_map/psum | solution.py:17
  216.9 8.7 %all-reduce.1 = (f32[7]{0:T(128)S(1)}, f32[7]{0:T(128)S(1)}) all-reduce(f32[7]{0:T(128)S(1)} %get-tuple-element.32, f32[7]{0:T(128)S(1)} %get-tuple-element.33), channel_id=1, replica_groups=mesh['dp_0'=4,'dp_1'=2,'dp_2'=2,'shard_0'=4,'shard_1'=2] {'shard_0'}, use_global_device_ids=true, to_apply=%region_17.18 | all-reduce | flops 14 | bytes 112 | tf_op jit(solution)/shard_map/psum | solution.py:17
  225.6 5.3 %all-reduce.3 = (f32[7]{0:T(128)S(1)}, f32[7]{0:T(128)S(1)}) all-reduce(f32[7]{0:T(128)S(1)} %get-tuple-element.26, f32[7]{0:T(128)S(1)} %get-tuple-element.27), channel_id=1, replica_groups=mesh['dp_0'=4,'dp_1'=2,'dp_2'=2,'shard_0'=4,'shard_1'=2] {'shard_1'}, use_global_device_ids=true, to_apply=%region_18.19 | all-reduce | flops 14 | bytes 112 | tf_op jit(solution)/shard_map/psum | solution.py:17
  230.9 0.2 select_reduce_fusion.2
  231.1 1.9 multiply_convert_fusion
  233.0 2.0 copy.70
  235.0 7.0 %all-to-all-start.1 = ((bf16[2,512,512]{2,0,1:T(2,128)(2,1)}), bf16[2,512,512]{2,0,1:T(2,128)(2,1)S(1)}, u32[]{:S(2)}, u32[]{:S(2)}) async-start(bf16[2,512,512]{2,0,1:T(2,128)(2,1)} %copy.70), calls=%async_computation.2 | async-start | bytes 2097152 | tf_op jit(solution)/shard_map/all_to_all | solution.py:77
  242.0 15.7 %all-to-all-done.1 = bf16[2,512,512]{2,0,1:T(2,128)(2,1)S(1)} async-done(((bf16[2,512,512]{2,0,1:T(2,128)(2,1)}), bf16[2,512,512]{2,0,1:T(2,128)(2,1)S(1)}, u32[]{:S(2)}, u32[]{:S(2)}) %all-to-all-start.1) | async-done | bytes 1048608 | tf_op jit(solution)/shard_map/all_to_all | solution.py:77
  257.7 0.2 copy.71
  257.9 0.1 copy.72
  258.0 0.6 gather_fusion.1
  258.6 0.1 broadcast_select_fusion.1
  258.7 3.3 stack.2
  261.9 5.3 %all-to-all-start.2 = ((bf16[16,11,32,512]{3,2,1,0:T(8,128)(2,1)}), bf16[16,11,32,512]{3,2,1,0:T(8,128)(2,1)}, u32[]{:S(2)}, u32[]{:S(2)}) async-start(bf16[16,11,32,512]{3,2,1,0:T(8,128)(2,1)} %stack.2), calls=%async_computation.3 | async-start | bytes 11534336 | tf_op jit(solution)/shard_map/all_to_all | solution.py:80
  267.2 6.1 %fusion = f32[2,1,512,512]{3,2,1,0:T(8,128)} fusion(f32[2,1,512,512]{3,2,1,0:T(8,128)} %param.12, f32[2,512,512]{2,1,0:T(8,128)S(1)} %bitcast.83), kind=kOutput, calls=%fused_computation.6 | convolution fusion | flops 3222798336 | bytes 6291456 | tf_op jit(solution)/shard_map/cji,cjk->cik/dot_general | solution.py:49
  273.4 0.0 copy-done.4
  273.4 5.0 %fusion.1 = f32[2,1,512,512]{3,2,1,0:T(8,128)} fusion(f32[2,1,512,512]{3,2,1,0:T(8,128)S(1)} %copy-done.4, f32[2,512,512]{2,1,0:T(8,128)S(1)} %bitcast.84), kind=kOutput, calls=%fused_computation.9 | convolution fusion | flops 3222798336 | bytes 6291456 | tf_op jit(solution)/shard_map/cij,ckj->cik/dot_general | solution.py:48
  278.4 55.3 %all-to-all-done.2 = bf16[16,11,32,512]{3,2,1,0:T(8,128)(2,1)} async-done(((bf16[16,11,32,512]{3,2,1,0:T(8,128)(2,1)}), bf16[16,11,32,512]{3,2,1,0:T(8,128)(2,1)}, u32[]{:S(2)}, u32[]{:S(2)}) %all-to-all-start.2) | async-done | bytes 5767200 | tf_op jit(solution)/shard_map/all_to_all | solution.py:80
  333.7 6.2 %copy.73 = bf16[16,11,32,512]{3,2,0,1:T(8,128)(2,1)} copy(bf16[16,11,32,512]{3,2,1,0:T(8,128)(2,1)} %all-to-all-done.2) | data formatting | bytes 11534336 | tf_op jit(solution)/shard_map/all_to_all | solution.py:80
  (17 shorter events, 0.1 us)
Async XLA Ops:
  7.2 185.8 %copy-start = (bf16[2,1,512,512]{3,2,1,0:T(8,128)(2,1)S(1)}, bf16[2,1,512,512]{3,2,1,0:T(8,128)(2,1)}, u32[]{:S(2)}) copy-start(bf16[2,1,512,512]{3,2,1,0:T(8,128)(2,1)} %param.15) | copy-start | bytes 3145732
  7.2 140.0 %reduce-scatter.2.cloned.1.call-start = ((), (), s32[]{:S(2)}) async-start(), calls=%async_computation.4 | async-start | bytes 12255232 | tf_op jit(solution)/shard_map/reduce_scatter | solution.py:39
  15.9 0.7 copy-start.6
  153.5 5.9 %copy-start.5 = (s32[88]{0:T(128)S(1)}, s32[88]{0:T(128)}, u32[]{:S(2)}) copy-start(s32[88]{0:T(128)} %param.10) | copy-start | bytes 1060
  153.5 32.9 %all-to-all-start = ((f32[16,2,32,512]{3,2,1,0:T(8,128)}), f32[16,2,32,512]{3,2,1,0:T(8,128)S(1)}, u32[]{:S(2)}, u32[]{:S(2)}) async-start(f32[16,2,32,512]{3,2,1,0:T(8,128)} %broadcast_select_fusion), calls=%async_computation.1 | async-start | bytes 4194304 | tf_op jit(solution)/shard_map/all_to_all | solution.py:46
  186.4 1.3 copy-start.2
  187.9 2.2 copy-start.3
  235.0 22.7 %all-to-all-start.1 = ((bf16[2,512,512]{2,0,1:T(2,128)(2,1)}), bf16[2,512,512]{2,0,1:T(2,128)(2,1)S(1)}, u32[]{:S(2)}, u32[]{:S(2)}) async-start(bf16[2,512,512]{2,0,1:T(2,128)(2,1)} %copy.70), calls=%async_computation.2 | async-start | bytes 2097152 | tf_op jit(solution)/shard_map/all_to_all | solution.py:77
  261.9 71.8 %all-to-all-start.2 = ((bf16[16,11,32,512]{3,2,1,0:T(8,128)(2,1)}), bf16[16,11,32,512]{3,2,1,0:T(8,128)(2,1)}, u32[]{:S(2)}, u32[]{:S(2)}) async-start(bf16[16,11,32,512]{3,2,1,0:T(8,128)(2,1)} %stack.2), calls=%async_computation.3 | async-start | bytes 11534336 | tf_op jit(solution)/shard_map/all_to_all | solution.py:80
  267.2 6.1 %copy-start.4 = (f32[2,1,512,512]{3,2,1,0:T(8,128)S(1)}, f32[2,1,512,512]{3,2,1,0:T(8,128)}, u32[]{:S(2)}) copy-start(f32[2,1,512,512]{3,2,1,0:T(8,128)} %param.11) | copy-start | bytes 6291460
  333.7 6.2 %copy-start.1 = (bf16[2,1,512,512]{3,2,1,0:T(8,128)(2,1)S(1)}, bf16[2,1,512,512]{3,2,1,0:T(8,128)(2,1)}, u32[]{:S(2)}) copy-start(bf16[2,1,512,512]{3,2,1,0:T(8,128)(2,1)} %param.15) | copy-start | bytes 3145732
Sparse Core Ops, SparseCore 0:
  16.0 131.0 reduce-scatter.1
